TPU v7x, 32 devices: a whole 2x2x4 slice. The times are simulated.
32 devices in a mesh: unit: 1, dp: 16 (over z, y, x), ens: 2 (over core).
Axes of the slice: x: 2, y: 2, z: 4, core: 2. Of those that a mesh axis runs over, the one named last changes fastest.
Arguments:
- samples_in: bfloat16 [4096, 4096], P(('unit', 'dp'), 'ens'), may hold values from -3 to 3, as said below
- second_samples_in: bfloat16 [4096, 4096], P(('unit', 'dp'), 'ens'), may hold values from -3 to 3, as said below
Outputs:
- scaled: float32 [4096, 4096], P('unit', ('ens', 'dp'))
- second_scaled: float32 [4096, 4096], P('unit', ('ens', 'dp'))
Inputs may be any that keep to these rules, and one draw needn't show every extreme that they name: samples_in holds numbers from -3 to 3. second_samples_in holds numbers from -3 to 3.
All inputs are finite; a program needn't handle non-finite values.
Results may differ from a plain program's by a relative error of at most 0.00035.
Values may be sent and summed in bfloat16 or wider, within the bound.
A program may use at most 128 MiB of HBM per device.

v0:
```python
import jax
import jax.numpy as jnp
from jax import lax
from jax.sharding import PartitionSpec as P


def per_device(samples_in, second_samples_in):
    moved_samples_in, moved_second_samples_in = (
        lax.all_to_all(samples_in, "dp", split_axis=1, concat_axis=0, tiled=True),
        lax.all_to_all(second_samples_in, "dp", split_axis=1, concat_axis=0, tiled=True),
    )
    wide_scaled = moved_samples_in.astype(jnp.float32)
    power_scaled = jnp.exp(wide_scaled)
    sum_scaled = jnp.sum(power_scaled, axis=0)
    scaled = power_scaled / sum_scaled * moved_samples_in.shape[0]
    wide_second_scaled = moved_second_samples_in.astype(jnp.float32)
    power_second_scaled = jnp.exp(wide_second_scaled)
    sum_second_scaled = jnp.sum(power_second_scaled, axis=0)
    second_scaled = power_second_scaled / sum_second_scaled * moved_second_samples_in.shape[0]
    return (scaled, second_scaled)


def solution(mesh):
    placed = (P(("unit", "dp"), "ens"), P(("unit", "dp"), "ens"))
    return jax.shard_map(
        per_device,
        mesh=mesh,
        in_specs=placed,
        out_specs=(P("unit", ("ens", "dp")), P("unit", ("ens", "dp"))),
        check_vma=False,
    )
```

profile of v0, /device:TPU:0, one launch (start us, length us, event | category | flops | bytes accessed | tf_op | source)
XLA Modules:
  0.0 67.5 jit_solution(8155692977923089948)
XLA Ops:
  0.6 0.0 copy-start
  0.6 1.2 %copy-done = bf16[256,2048]{1,0:T(8,128)(2,1)S(1)} copy-done((bf16[256,2048]{1,0:T(8,128)(2,1)S(1)}, bf16[256,2048]{1,0:T(8,128)(2,1)}, u32[]{:S(2)}) %copy-start) | copy-done | bytes 1048600
  1.9 0.0 copy-start.1
  1.9 1.2 %copy_bitcast_fusion = bf16[256,16,128]{2,0,1:T(8,128)(2,1)} fusion(bf16[256,2048]{1,0:T(8,128)(2,1)S(1)} %copy-done), kind=kLoop, calls=%fused_computation.6 | loop fusion | bytes 2097152 | tf_op jit(solution)/shard_map/all_to_all | solution.py:10
  3.1 8.4 %all-to-all-start.1 = ((bf16[256,16,128]{2,0,1:T(8,128)(2,1)}), bf16[256,16,128]{2,0,1:T(8,128)(2,1)S(1)}, u32[]{:S(2)}, u32[]{:S(2)}) async-start(bf16[256,16,128]{2,0,1:T(8,128)(2,1)} %copy_bitcast_fusion), calls=%async_computation.1 | async-start | bytes 2097152 | tf_op jit(solution)/shard_map/all_to_all | solution.py:10
  11.5 0.0 copy-done.1
  11.5 1.2 %copy_bitcast_fusion.1 = bf16[256,16,128]{2,0,1:T(8,128)(2,1)} fusion(bf16[256,2048]{1,0:T(8,128)(2,1)S(1)} %copy-done.1), kind=kLoop, calls=%fused_computation.7 | loop fusion | bytes 2097152 | tf_op jit(solution)/shard_map/all_to_all | solution.py:9
  12.7 23.3 %all-to-all-done.1 = bf16[256,16,128]{2,0,1:T(8,128)(2,1)S(1)} async-done(((bf16[256,16,128]{2,0,1:T(8,128)(2,1)}), bf16[256,16,128]{2,0,1:T(8,128)(2,1)S(1)}, u32[]{:S(2)}, u32[]{:S(2)}) %all-to-all-start.1) | async-done | bytes 1048608 | tf_op jit(solution)/shard_map/all_to_all | solution.py:10
  36.1 5.9 %all-to-all-start = ((bf16[256,16,128]{2,0,1:T(8,128)(2,1)}), bf16[256,16,128]{2,0,1:T(8,128)(2,1)S(1)}, u32[]{:S(2)}, u32[]{:S(2)}) async-start(bf16[256,16,128]{2,0,1:T(8,128)(2,1)} %copy_bitcast_fusion.1), calls=%async_computation | async-start | bytes 2097152 | tf_op jit(solution)/shard_map/all_to_all | solution.py:9
  42.0 0.6 fusion.3
  42.6 1.5 %fusion = f32[4096,128]{1,0:T(8,128)} fusion(f32[256,16,128]{2,0,1:T(8,128)S(1)} %get-tuple-element.3, f32[128]{0:T(128)S(1)} %get-tuple-element.2), kind=kLoop, calls=%fused_computation.1 | loop fusion | flops 1048576 | bytes 4194816 | tf_op jit(solution)/shard_map/mul | solution.py:19
  44.1 21.4 %all-to-all-done = bf16[256,16,128]{2,0,1:T(8,128)(2,1)S(1)} async-done(((bf16[256,16,128]{2,0,1:T(8,128)(2,1)}), bf16[256,16,128]{2,0,1:T(8,128)(2,1)S(1)}, u32[]{:S(2)}, u32[]{:S(2)}) %all-to-all-start) | async-done | bytes 1048608 | tf_op jit(solution)/shard_map/all_to_all | solution.py:9
  65.5 0.6 fusion.2
  66.0 1.5 %fusion.1 = f32[4096,128]{1,0:T(8,128)} fusion(f32[256,16,128]{2,0,1:T(8,128)S(1)} %get-tuple-element.5, f32[128]{0:T(128)S(1)} %get-tuple-element.4), kind=kLoop, calls=%fused_computation.3 | loop fusion | flops 1048576 | bytes 4194816 | tf_op jit(solution)/shard_map/mul | solution.py:15
Async XLA Ops:
  0.6 1.2 %copy-start = (bf16[256,2048]{1,0:T(8,128)(2,1)S(1)}, bf16[256,2048]{1,0:T(8,128)(2,1)}, u32[]{:S(2)}) copy-start(bf16[256,2048]{1,0:T(8,128)(2,1)} %param.3) | copy-start | bytes 3145732
  1.9 9.6 %copy-start.1 = (bf16[256,2048]{1,0:T(8,128)(2,1)S(1)}, bf16[256,2048]{1,0:T(8,128)(2,1)}, u32[]{:S(2)}) copy-start(bf16[256,2048]{1,0:T(8,128)(2,1)} %param.2) | copy-start | bytes 3145732
  3.1 33.0 %all-to-all-start.1 = ((bf16[256,16,128]{2,0,1:T(8,128)(2,1)}), bf16[256,16,128]{2,0,1:T(8,128)(2,1)S(1)}, u32[]{:S(2)}, u32[]{:S(2)}) async-start(bf16[256,16,128]{2,0,1:T(8,128)(2,1)} %copy_bitcast_fusion), calls=%async_computation.1 | async-start | bytes 2097152 | tf_op jit(solution)/shard_map/all_to_all | solution.py:10
  36.1 29.4 %all-to-all-start = ((bf16[256,16,128]{2,0,1:T(8,128)(2,1)}), bf16[256,16,128]{2,0,1:T(8,128)(2,1)S(1)}, u32[]{:S(2)}, u32[]{:S(2)}) async-start(bf16[256,16,128]{2,0,1:T(8,128)(2,1)} %copy_bitcast_fusion.1), calls=%async_computation | async-start | bytes 2097152 | tf_op jit(solution)/shard_map/all_to_all | solution.py:9
where the time goes:
time: 68.1 us; the launch traced here: 67.5 us
  waiting for transfers between devices  44.7 us (66%)
  starting transfers between devices  14.3 us (21%)
  other arithmetic  4.07 us (6%)
  local copies, waits for them, and re-layouts  3.71 us (5%)
    all_to_all x1, waiting for transfers between devices, per_device(): lax.all_to_all(second_samples_in, 'dp', split_axis=1, concat_axis=0, tile...  23.3 us
    all_to_all x1, waiting for transfers between devices, per_device(): lax.all_to_all(samples_in, 'dp', split_axis=1, concat_axis=0, tiled=True)  21.4 us
    all_to_all x1, starting transfers between devices, per_device(): lax.all_to_all(second_samples_in, 'dp', split_axis=1, concat_axis=0, tile...  8.37 us
    all_to_all x1, starting transfers between devices, per_device(): lax.all_to_all(samples_in, 'dp', split_axis=1, concat_axis=0, tiled=True)  5.92 us
    mul x1, other arithmetic, per_device(): power_second_scaled / sum_second_scaled * moved_second_samples_in.shape[0]  1.47 us
    mul x1, other arithmetic, per_device(): scaled = power_scaled / sum_scaled * moved_samples_in.shape[0]  1.47 us
  transfers between devices with their start and end apart: 2, of which 2 were waited for; matrix products, arithmetic and copies ran while one was open for 5% of the time, Pallas kernels for 0%

commit v1 on v0

v1 whole, which is shorter than its diff:
```python
import functools

import jax
import jax.numpy as jnp
from jax import lax
from jax.experimental import pallas as pl
from jax.experimental.pallas import tpu as pltpu
from jax.sharding import PartitionSpec as P

MESH = pl.DeviceIdType.MESH


def send_orders(n):
    quarter = max(n // 4, 1)
    near = list(range(1, quarter))
    side = list(range(quarter, n // 2))
    far = [k for i in range(quarter) for k in (3 * quarter + i, 2 * quarter + i)]
    outer = side + far[:2] + near + far[2:]
    inner = far[:2] + near
    rest, sides = far[2:], list(side)
    while rest or sides:
        inner += rest[:2]
        rest = rest[2:]
        inner += sides[:1]
        sides = sides[1:]
    waits = near + side + far
    return outer, inner, waits


def partner(me, k, n):
    total, bit = 0, 1
    while bit < n:
        total = total + ((me // bit + k // bit) % 2) * bit
        bit *= 2
    return total


def exchange(n, x0, x1, p0, p1, scale, in0, in1, held, load_sem, send_sem, recv_sem):
    xs, ins, ps = (x0, x1), (in0, in1), (p0, p1)
    rows, width = x0.shape[0], x0.shape[1] // n
    me = lax.axis_index("dp")
    outer_order, inner_order, wait_order = send_orders(n)
    quarter_of_me = me * 4 // n
    inner = (quarter_of_me + 1) // 2 % 2

    loads = [pltpu.make_async_copy(xs[a], ins[a], load_sem.at[a]) for a in range(2)]
    for load in loads:
        load.start()

    barrier = pltpu.get_barrier_semaphore()
    for k in range(1, n):
        pl.semaphore_signal(barrier, inc=1, device_id={"dp": partner(me, k, n)}, device_id_type=MESH)
    pl.semaphore_wait(barrier, n - 1)

    for load in loads:
        load.wait()

    def copy(a, k, to, at):
        return pltpu.make_async_remote_copy(
            src_ref=ins[a].at[:, pl.ds(pl.multiple_of(to * width, width), width)],
            dst_ref=held.at[a, pl.ds(pl.multiple_of(at * rows, rows), rows), :],
            send_sem=send_sem.at[a, k],
            recv_sem=recv_sem.at[a, k],
            device_id={"dp": to},
            device_id_type=MESH,
        )

    for from_outer, from_inner in zip(outer_order, inner_order):
        k = from_outer + inner * (from_inner - from_outer)
        to = partner(me, k, n)
        for a in range(2):
            copy(a, k, to, me).start()

    def raised(block):
        power = jnp.exp(block.astype(jnp.float32))
        return power, jnp.sum(power.reshape(rows // 8, 8, width), axis=0)

    own_rows = pl.ds(pl.multiple_of(me * rows, rows), rows)
    own_columns = pl.ds(pl.multiple_of(me * width, width), width)
    sums = []
    for a in range(2):
        power, part = raised(ins[a][:, own_columns])
        ps[a][own_rows, :] = power
        sums.append(part)
    for k in wait_order:
        source = partner(me, k, n)
        its_rows = pl.ds(pl.multiple_of(source * rows, rows), rows)
        for a in range(2):
            copy(a, k, source, source).wait_recv()
            power, part = raised(held[a, its_rows, :])
            ps[a][its_rows, :] = power
            sums[a] = sums[a] + part
    for a in range(2):
        scale[a] = jnp.broadcast_to(n * rows / jnp.sum(sums[a], axis=0, keepdims=True), (8, width))
    for k in wait_order:
        to = partner(me, k, n)
        for a in range(2):
            copy(a, k, to, me).wait_send()


def per_device(n, samples_in, second_samples_in):
    rows, wide = samples_in.shape
    width = wide // n
    in_hbm = pl.BlockSpec(memory_space=pltpu.HBM)
    scratch_bytes = 4 * rows * wide * samples_in.dtype.itemsize
    in_vmem = pl.BlockSpec(memory_space=pltpu.VMEM)
    power_scaled, power_second_scaled, scale = pl.pallas_call(
        functools.partial(exchange, n),
        out_shape=(
            pltpu.VMEM((n * rows, width), jnp.float32),
            pltpu.VMEM((n * rows, width), jnp.float32),
            pltpu.VMEM((2, 8, width), jnp.float32),
        ),
        in_specs=[in_hbm] * 2,
        out_specs=(in_vmem,) * 3,
        scratch_shapes=[
            pltpu.VMEM((rows, wide), samples_in.dtype),
            pltpu.VMEM((rows, wide), samples_in.dtype),
            pltpu.VMEM((2, n * rows, width), samples_in.dtype),
            pltpu.SemaphoreType.DMA((2,)),
            pltpu.SemaphoreType.DMA((2, n)),
            pltpu.SemaphoreType.DMA((2, n)),
        ],
        compiler_params=pltpu.CompilerParams(
            collective_id=0,
            has_side_effects=True,
            vmem_limit_bytes=scratch_bytes + 2**21,
        ),
    )(samples_in, second_samples_in)
    return power_scaled * scale[0, :1], power_second_scaled * scale[1, :1]


def solution(mesh):
    placed = (P(("unit", "dp"), "ens"), P(("unit", "dp"), "ens"))
    return jax.shard_map(
        functools.partial(per_device, mesh.shape["dp"]),
        mesh=mesh,
        in_specs=placed,
        out_specs=(P("unit", ("ens", "dp")), P("unit", ("ens", "dp"))),
        check_vma=False,
    )
```

time: 68.1 us -> 60.7 us (0.89)
  Pallas kernels: 0 us -> 55.1 us
  waiting for transfers between devices: 44.7 us -> 0 us
  starting transfers between devices: 14.3 us -> 0 us
  other arithmetic: 4.07 us -> 2.28 us
  local copies, waits for them, and re-layouts: 3.71 us -> 2.45 us
    pallas_call x0 -> x1, Pallas kernels: none -> 55.1 us  [per_device(): pl.pallas_call(functools.partial(exchange, n), out_shape=(pltpu.VMEM((n *...]
    all_to_all x2 -> x0, waiting for transfers between devices: 44.7 us -> none  [the longest x1 23.3 us: per_device(): lax.all_to_all(second_samples_in, 'dp', split_axis=1, concat_axis=0, tile...]
    all_to_all x2 -> x0, starting transfers between devices: 14.3 us -> none  [the longest x1 8.37 us: per_device(): lax.all_to_all(second_samples_in, 'dp', split_axis=1, concat_axis=0, tile...]
    all_to_all x2 -> x0, local copies, waits for them, and re-layouts: 2.49 us -> none  [the longest x1 1.24 us: per_device(): lax.all_to_all(samples_in, 'dp', split_axis=1, concat_axis=0, tiled=True)]
    unnamed x4, local copies, waits for them, and re-layouts: 1.23 us -> 2.44 us
    reduce_sum x2 -> x0, other arithmetic: 1.12 us -> none  [the longest x1 0.56 us: per_device(): sum_second_scaled = jnp.sum(power_second_scaled, axis=0)]
    mul x2 -> x1, other arithmetic: 2.94 us -> 2.28 us  [per_device(): return (power_scaled * scale[0, :1], power_second_scaled * scale[1, :1])]
  transfers between devices with their start and end apart: 2 -> 0, of which waited for: 2 -> 0; matrix products, arithmetic and copies ran while one was open for 5% -> 0% of each run, Pallas kernels for 0% -> 0%
where the time goes in v1:
time: 60.7 us; the launch traced here: 60.5 us
  Pallas kernels  55.1 us (91%)
  local copies, waits for them, and re-layouts  2.45 us (4%)
  other arithmetic  2.28 us (4%)
  between operations  0.65 us (1%)
    pallas_call x1, Pallas kernels, per_device(): pl.pallas_call(functools.partial(exchange, n), out_shape=(pltpu.VMEM((n *...  55.1 us
    unnamed x4, local copies, waits for them, and re-layouts  2.44 us
    mul x1, other arithmetic, per_device(): return (power_scaled * scale[0, :1], power_second_scaled * scale[1, :1])  2.28 us

profile of v1, /device:TPU:0, one launch (start us, length us, event | category | flops | bytes accessed | tf_op | source)
XLA Modules:
  0.0 60.5 jit_solution(6236753109580446593)
XLA Ops:
  0.6 0.0 copy-start
  0.6 1.2 %copy-done = bf16[256,2048]{1,0:T(8,128)(2,1)S(1)} copy-done((bf16[256,2048]{1,0:T(8,128)(2,1)S(1)}, bf16[256,2048]{1,0:T(8,128)(2,1)}, u32[]{:S(2)}) %copy-start) | copy-done | bytes 1048600
  1.9 0.0 copy-start.1
  1.9 1.2 %copy-done.1 = bf16[256,2048]{1,0:T(8,128)(2,1)S(1)} copy-done((bf16[256,2048]{1,0:T(8,128)(2,1)S(1)}, bf16[256,2048]{1,0:T(8,128)(2,1)}, u32[]{:S(2)}) %copy-start.1) | copy-done | bytes 1048600
  3.1 55.1 %shard_map.41 = (f32[4096,128]{1,0:T(8,128)S(1)}, f32[4096,128]{1,0:T(8,128)S(1)}, f32[2,8,128]{2,1,0:T(8,128)S(1)}) custom-call(bf16[256,2048]{1,0:T(8,128)(2,1)S(1)} %copy-done, bf16[256,2048]{1,0:T(8,128)(2,1)S(1)} %copy-done.1), custom_call_target="tpu_custom_call" | custom-call | tf_op jit(solution)/shard_map/pallas_call | solution.py:107
  58.2 2.3 %broadcast_multiply_fusion = (f32[4096,128]{1,0:T(8,128)}, f32[4096,128]{1,0:T(8,128)}) fusion(f32[4096,128]{1,0:T(8,128)S(1)} %get-tuple-element.7, f32[128]{0:T(128)S(1)} %get-tuple-element.8, f32[4096,128]{1,0:T(8,128)S(1)} %get-tuple-element.5, f32[128]{0:T(128)S(1)} %get-tuple-element.9), kind=kLoop, calls=%fused_computation | loop fusion | flops 1048576 | bytes 8389632 | tf_op jit(solution)/shard_map/mul | solution.py:130
  (1 shorter events, 0.0 us)
Async XLA Ops:
  0.6 1.2 %copy-start = (bf16[256,2048]{1,0:T(8,128)(2,1)S(1)}, bf16[256,2048]{1,0:T(8,128)(2,1)}, u32[]{:S(2)}) copy-start(bf16[256,2048]{1,0:T(8,128)(2,1)} %x0.1) | copy-start | bytes 3145732
  1.9 1.2 %copy-start.1 = (bf16[256,2048]{1,0:T(8,128)(2,1)S(1)}, bf16[256,2048]{1,0:T(8,128)(2,1)}, u32[]{:S(2)}) copy-start(bf16[256,2048]{1,0:T(8,128)(2,1)} %x1.1) | copy-start | bytes 3145732

commit v2 on v1

--- a/solution.py
+++ b/solution.py
@@ -102,7 +102,7 @@
     rows, wide = samples_in.shape
     width = wide // n
     in_hbm = pl.BlockSpec(memory_space=pltpu.HBM)
-    scratch_bytes = 4 * rows * wide * samples_in.dtype.itemsize
+    out_bytes = 2 * n * rows * width * 4
     in_vmem = pl.BlockSpec(memory_space=pltpu.VMEM)
     power_scaled, power_second_scaled, scale = pl.pallas_call(
         functools.partial(exchange, n),
@@ -124,7 +124,7 @@
         compiler_params=pltpu.CompilerParams(
             collective_id=0,
             has_side_effects=True,
-            vmem_limit_bytes=scratch_bytes + 2**21,
+            vmem_limit_bytes=67043328 - out_bytes - 2**19,
         ),
     )(samples_in, second_samples_in)
     return power_scaled * scale[0, :1], power_second_scaled * scale[1, :1]

time: 60.7 us -> 58.9 us (0.970)
  local copies, waits for them, and re-layouts: 2.45 us -> 0.01 us
  Pallas kernels: 55.1 us -> 55.9 us
    unnamed x4 -> x0, local copies, waits for them, and re-layouts: 2.44 us -> none
    pallas_call x1, Pallas kernels: 55.1 us -> 55.9 us  [per_device(): pl.pallas_call(functools.partial(exchange, n), out_shape=(pltpu.VMEM((n *...]
where the time goes in v2:
time: 58.9 us; the launch traced here: 58.8 us
  Pallas kernels  55.9 us (95%)
  other arithmetic  2.28 us (4%)
  between operations  0.65 us (1%)
    pallas_call x1, Pallas kernels, per_device(): pl.pallas_call(functools.partial(exchange, n), out_shape=(pltpu.VMEM((n *...  55.9 us
    mul x1, other arithmetic, per_device(): return (power_scaled * scale[0, :1], power_second_scaled * scale[1, :1])  2.28 us

profile of v2, /device:TPU:0, one launch (start us, length us, event | category | flops | bytes accessed | tf_op | source)
XLA Modules:
  0.0 58.8 jit_solution(13420354037364392775)
XLA Ops:
  0.6 55.9 %shard_map.41 = (f32[4096,128]{1,0:T(8,128)S(1)}, f32[4096,128]{1,0:T(8,128)S(1)}, f32[2,8,128]{2,1,0:T(8,128)S(1)}) custom-call(bf16[256,2048]{1,0:T(8,128)(2,1)} %x0.1, bf16[256,2048]{1,0:T(8,128)(2,1)} %x1.1), custom_call_target="tpu_custom_call" | custom-call | tf_op jit(solution)/shard_map/pallas_call | solution.py:107
  56.5 2.3 %broadcast_multiply_fusion = (f32[4096,128]{1,0:T(8,128)}, f32[4096,128]{1,0:T(8,128)}) fusion(f32[4096,128]{1,0:T(8,128)S(1)} %get-tuple-element.7, f32[128]{0:T(128)S(1)} %get-tuple-element.8, f32[4096,128]{1,0:T(8,128)S(1)} %get-tuple-element.5, f32[128]{0:T(128)S(1)} %get-tuple-element.9), kind=kLoop, calls=%fused_computation | loop fusion | flops 1048576 | bytes 8389632 | tf_op jit(solution)/shard_map/mul | solution.py:130
  (1 shorter events, 0.0 us)

commit v3 on v2

--- a/solution.py
+++ b/solution.py
@@ -14,15 +14,20 @@
     quarter = max(n // 4, 1)
     near = list(range(1, quarter))
     side = list(range(quarter, n // 2))
-    far = [k for i in range(quarter) for k in (3 * quarter + i, 2 * quarter + i)]
+    to_own_kind = list(range(3 * quarter, n))
+    to_other_kind = list(range(2 * quarter, 3 * quarter))
+
+    def far_first_to_outer(outer_bound, inner_bound):
+        half = (quarter + 1) // 2
+        far = [k for pair in zip(outer_bound, inner_bound) for k in pair][: 2 * half]
+        return far + outer_bound[half:] + inner_bound[half:]
+
+    far = far_first_to_outer(to_own_kind, to_other_kind)
     outer = side + far[:2] + near + far[2:]
-    inner = far[:2] + near
-    rest, sides = far[2:], list(side)
-    while rest or sides:
-        inner += rest[:2]
-        rest = rest[2:]
-        inner += sides[:1]
-        sides = sides[1:]
+    rest = far_first_to_outer(to_other_kind, to_own_kind)
+    inner, rest = rest[:2] + near, rest[2:]
+    for i in range(max(len(rest), len(side))):
+        inner += side[i : i + 1] + rest[i : i + 1]
     waits = near + side + far
     return outer, inner, waits
 

time: 58.9 us -> 54.9 us (0.932)
  the two profiles are of different devices: /device:TPU:0 before, /device:TPU:16 now
where the time goes in v3:
time: 54.9 us; the launch traced here: 54.7 us
  Pallas kernels  51.8 us (94%)
  other arithmetic  2.28 us (4%)
  between operations  0.65 us (1%)
    pallas_call x1, Pallas kernels, per_device(): pl.pallas_call(functools.partial(exchange, n), out_shape=(pltpu.VMEM((n *...  51.8 us
    mul x1, other arithmetic, per_device(): return (power_scaled * scale[0, :1], power_second_scaled * scale[1, :1])  2.28 us

profile of v3, /device:TPU:16, one launch (start us, length us, event | category | flops | bytes accessed | tf_op | source)
XLA Modules:
  0.0 54.7 jit_solution(13941882079056469534)
XLA Ops:
  0.6 51.8 %shard_map.41 = (f32[4096,128]{1,0:T(8,128)S(1)}, f32[4096,128]{1,0:T(8,128)S(1)}, f32[2,8,128]{2,1,0:T(8,128)S(1)}) custom-call(bf16[256,2048]{1,0:T(8,128)(2,1)} %x0.1, bf16[256,2048]{1,0:T(8,128)(2,1)} %x1.1), custom_call_target="tpu_custom_call" | custom-call | tf_op jit(solution)/shard_map/pallas_call | solution.py:112
  52.5 2.3 %broadcast_multiply_fusion = (f32[4096,128]{1,0:T(8,128)}, f32[4096,128]{1,0:T(8,128)}) fusion(f32[4096,128]{1,0:T(8,128)S(1)} %get-tuple-element.7, f32[128]{0:T(128)S(1)} %get-tuple-element.8, f32[4096,128]{1,0:T(8,128)S(1)} %get-tuple-element.5, f32[128]{0:T(128)S(1)} %get-tuple-element.9), kind=kLoop, calls=%fused_computation | loop fusion | flops 1048576 | bytes 8389632 | tf_op jit(solution)/shard_map/mul | solution.py:135
  (1 shorter events, 0.0 us)

commit v4 on v3

--- a/solution.py
+++ b/solution.py
@@ -18,9 +18,7 @@
     to_other_kind = list(range(2 * quarter, 3 * quarter))
 
     def far_first_to_outer(outer_bound, inner_bound):
-        half = (quarter + 1) // 2
-        far = [k for pair in zip(outer_bound, inner_bound) for k in pair][: 2 * half]
-        return far + outer_bound[half:] + inner_bound[half:]
+        return [k for pair in zip(outer_bound, inner_bound) for k in pair]
 
     far = far_first_to_outer(to_own_kind, to_other_kind)
     outer = side + far[:2] + near + far[2:]

time: 54.9 us -> 55.4 us (level)
  the two profiles are of different devices: /device:TPU:16 before, /device:TPU:0 now
where the time goes in v4:
time: 55.4 us; the launch traced here: 55.3 us
  Pallas kernels  52.3 us (94%)
  other arithmetic  2.28 us (4%)
  between operations  0.65 us (1%)
    pallas_call x1, Pallas kernels, per_device(): pl.pallas_call(functools.partial(exchange, n), out_shape=(pltpu.VMEM((n *...  52.3 us
    mul x1, other arithmetic, per_device(): return (power_scaled * scale[0, :1], power_second_scaled * scale[1, :1])  2.28 us

profile of v4, /device:TPU:0, one launch (start us, length us, event | category | flops | bytes accessed | tf_op | source)
XLA Modules:
  0.0 55.3 jit_solution(11334953982896729040)
XLA Ops:
  0.6 52.3 %shard_map.41 = (f32[4096,128]{1,0:T(8,128)S(1)}, f32[4096,128]{1,0:T(8,128)S(1)}, f32[2,8,128]{2,1,0:T(8,128)S(1)}) custom-call(bf16[256,2048]{1,0:T(8,128)(2,1)} %x0.1, bf16[256,2048]{1,0:T(8,128)(2,1)} %x1.1), custom_call_target="tpu_custom_call" | custom-call | tf_op jit(solution)/shard_map/pallas_call | solution.py:110
  53.0 2.3 %broadcast_multiply_fusion = (f32[4096,128]{1,0:T(8,128)}, f32[4096,128]{1,0:T(8,128)}) fusion(f32[4096,128]{1,0:T(8,128)S(1)} %get-tuple-element.7, f32[128]{0:T(128)S(1)} %get-tuple-element.8, f32[4096,128]{1,0:T(8,128)S(1)} %get-tuple-element.5, f32[128]{0:T(128)S(1)} %get-tuple-element.9), kind=kLoop, calls=%fused_computation | loop fusion | flops 1048576 | bytes 8389632 | tf_op jit(solution)/shard_map/mul | solution.py:133
  (1 shorter events, 0.0 us)
